TPU v7x, 512 devices: a whole 4x4x16 slice. The times are simulated.
512 devices in a mesh: batch: 16 (over y, x), ctx: 32 (over z, core).
Axes of the slice: x: 4, y: 4, z: 16, core: 2. Of those that a mesh axis runs over, the one named last changes fastest.
Arguments:
- asked_for: bfloat16 [16, 4096, 64, 64], P('batch', 'ctx'), may hold values from -6 to 6
- offered: bfloat16 [16, 4096, 64, 64], P('batch', 'ctx'), may hold values from -6 to 6
- contents: bfloat16 [16, 4096, 64, 64], P('batch', 'ctx'), may hold values from -6 to 6
- out_weight: bfloat16 [4096, 4096], P('batch'), may hold values from -0.09375 to 0.09375
Outputs:
- layer_out: bfloat16 [16, 4096, 4096], P('batch', 'ctx')
All inputs are finite; a program needn't handle non-finite values.
Results may differ from a plain program's by a relative error of at most 0.006.
Values may be sent and summed in bfloat16 or wider, within the bound.
A program may use at most 128 MiB of HBM per device.

v0:
```python
import jax
import jax.numpy as jnp
from jax import lax
from jax.sharding import PartitionSpec as P


def packed_total(arrays, axis):
    ends = [0]
    for a in arrays:
        ends.append(ends[-1] + a.size)
    total = lax.psum(jnp.concatenate([a.ravel() for a in arrays]), axis)
    return tuple((total[b:e].reshape(a.shape) for a, b, e in zip(arrays, ends, ends[1:])))


def to_features(values):
    wide = values.astype(jnp.float32)
    return jax.nn.softplus(wide).astype(jnp.bfloat16)


def after_reading(read, count):
    result = read * count**0.5
    return result.astype(jnp.bfloat16)


def look_up(features, state, mass):
    top = jnp.einsum(
        "bthd,bhde->bthe", features, state.astype(jnp.bfloat16), preferred_element_type=jnp.float32
    )
    bottom = jnp.einsum("bthd,bhd->bth", features.astype(jnp.float32), mass)
    return top / (bottom + 0.001)[..., None]


def shards(asked_for, offered, contents, out_weight):
    query_feature, key_feature = (to_features(asked_for), to_features(offered))
    count = asked_for.shape[1] * lax.axis_size("ctx")
    part_state = jnp.einsum(
        "bthd,bthe->bhde", key_feature, contents, preferred_element_type=jnp.float32
    )
    part_mass = jnp.sum(key_feature.astype(jnp.float32), axis=1)
    state, mass = packed_total((part_state, part_mass), "ctx")
    read = look_up(query_feature, state / count, mass / count)
    mixed = after_reading(read, count)
    mixed = mixed.reshape(mixed.shape[0], mixed.shape[1], -1)
    return jnp.einsum(
        "btw,wv->btv",
        mixed,
        lax.all_gather(out_weight, "batch", axis=0, tiled=True),
        preferred_element_type=jnp.float32,
    ).astype(jnp.bfloat16)


def solution(mesh):
    in_specs = (
        P("batch", "ctx", None, None),
        P("batch", "ctx", None, None),
        P("batch", "ctx", None, None),
        P("batch", None),
    )
    out_specs = P("batch", "ctx", None)
    return jax.shard_map(shards, mesh=mesh, in_specs=in_specs, out_specs=out_specs, check_vma=False)
```

profile of v0, /device:TPU:1, one launch (start us, length us, event | category | flops | bytes accessed | tf_op | source)
XLA Modules:
  0.0 263.6 jit_solution(13410124035713011407)
XLA Ops:
  7.4 0.0 copy-start
  7.4 0.0 all-reduce.2.cloned.1.call-start
  7.4 2.6 convert_reduce_fusion
  10.0 0.0 copy-done
  10.0 3.9 %fusion.15 = f32[64,64,64]{2,1,0:T(8,128)} fusion(bf16[1,128,64,64]{1,3,2,0:T(8,128)(2,1)S(1)} %copy-done, bf16[1,128,64,64]{1,3,2,0:T(8,128)(2,1)} %param.5), kind=kOutput, calls=%fused_computation.26 | convolution fusion | flops 71303168 | bytes 3145728 | tf_op jit(solution)/shard_map/bthd,bthe->bhde/dot_general | solution.py:36
  13.8 1.8 reshape.70
  15.7 0.1 reshape.71
  15.7 1.1 pad_maximum_fusion
  16.8 0.0 all-reduce.2.cloned.1.call-update
  16.8 0.0 all-gather.2.cloned.1.call-start
  16.9 0.5 all-gather.2.cloned.1.call-update
  17.4 218.0 %all-reduce.2.cloned.1.call-done = f32[266240]{0:T(1024)} async-done(((f32[266240]{0:T(1024)}), f32[266240]{0:T(1024)}) %all-reduce.2.cloned.1.call-update) | async-done | bytes 1064976 | tf_op jit(solution)/shard_map/psum | solution.py:11
  235.4 1.3 fusion.14
  236.7 0.4 convert_element_type.38
  237.1 0.7 slice_multiply_fusion.1
  237.8 0.1 reshape.74
  237.9 0.0 copy-start.1
  237.9 2.6 fusion.19
  240.5 0.0 copy-done.1
  240.5 1.6 fusion.12
  242.1 0.0 all-gather.2.cloned.1.call-done
  242.1 14.0 %fusion = bf16[1,128,4096]{2,1,0:T(8,128)(2,1)} fusion(bf16[128,4096]{0,1:T(8,128)(2,1)S(1)} %bitcast.34, bf16[4096,4096]{1,0:T(8,128)(2,1)} %all-gather.2.cloned.1.call-done), kind=kOutput, calls=%fused_computation.3 | convolution fusion | flops 4295491584 | bytes 35651584 | tf_op jit(solution)/shard_map/btw,wv->btv/dot_general | solution.py:44
  (1 shorter events, 0.0 us)
Async XLA Ops:
  7.4 2.6 copy-start
  7.4 228.0 %all-reduce.2.cloned.1.call-start = ((), (), s32[]{:S(2)}) async-start(), calls=%async_computation | async-start | bytes 2129920 | tf_op jit(solution)/shard_map/psum | solution.py:11
  16.8 225.3 %all-gather.2.cloned.1.call-start = ((), (), s32[]{:S(2)}) async-start(), calls=%async_computation.1 | async-start | bytes 35651584 | tf_op jit(solution)/shard_map/all_gather | solution.py:47
  237.9 2.6 copy-start.1
Sparse Core Ops, SparseCore 0:
  17.0 218.3 all-reduce.1
Sparse Core Ops, SparseCore 1:
  20.3 217.2 all-gather.1
where the time goes:
time: 264 us
  waiting for transfers between devices  219 us (83%)
  matrix products  22.1 us (8%)
  between operations  14.9 us (6%)
  other arithmetic  5.7 us (2%)
    psum x1, waiting for transfers between devices, packed_total(): total = lax.psum(jnp.concatenate([a.ravel() for a in arrays]), axis)  218 us
    dot_general x1, matrix products, shards(): jnp.einsum('btw,wv->btv', mixed, lax.all_gather(out_weight, 'batch', axis...  14 us
  transfers between devices with their start and end apart: 2, of which 1 were waited for; matrix products, arithmetic and copies ran while one was open for 3% of the time, Pallas kernels for 0%

commit v1 on v0

--- a/solution.py
+++ b/solution.py
@@ -8,7 +8,7 @@
     ends = [0]
     for a in arrays:
         ends.append(ends[-1] + a.size)
-    total = lax.psum(jnp.concatenate([a.ravel() for a in arrays]), axis)
+    total = jnp.sum(lax.all_gather(jnp.concatenate([a.ravel() for a in arrays]), axis), axis=0)
     return tuple((total[b:e].reshape(a.shape) for a, b, e in zip(arrays, ends, ends[1:])))
 
 

time: 264 us -> 447 us (1.69)
  waiting for transfers between devices: 219 us -> 356 us
  local copies, waits for them, and re-layouts: 2.35 us -> 35.3 us
  other arithmetic: 5.7 us -> 20.3 us
    psum x1 -> x0, waiting for transfers between devices: 218 us -> none  [packed_total(): total = lax.psum(jnp.concatenate([a.ravel() for a in arrays]), axis)]
    all_gather x0 -> x1, waiting for transfers between devices: none -> 199 us  [packed_total(): lax.all_gather(jnp.concatenate([a.ravel() for a in arrays]), axis)]
    all_gather x1, waiting for transfers between devices: 0.03 us -> 157 us  [shards(): lax.all_gather(out_weight, 'batch', axis=0, tiled=True)]
    all_gather x0 -> x1, local copies, waits for them, and re-layouts: none -> 34.4 us  [packed_total(): lax.all_gather(jnp.concatenate([a.ravel() for a in arrays]), axis)]
    reduce_sum x0 -> x1, other arithmetic: none -> 16.6 us  [packed_total(): jnp.sum(lax.all_gather(jnp.concatenate([a.ravel() for a in arrays]), axis...]
  transfers between devices with their start and end apart: 2 -> 2, of which waited for: 1 -> 2; matrix products, arithmetic and copies ran while one was open for 3% -> 12% of each run, Pallas kernels for 0% -> 0%
where the time goes in v1:
time: 447 us; the launch traced here: 446 us
  waiting for transfers between devices  356 us (80%)
  local copies, waits for them, and re-layouts  35.3 us (8%)
  matrix products  20.9 us (5%)
  other arithmetic  20.3 us (5%)
  between operations  13.5 us (3%)
    all_gather x1, waiting for transfers between devices, packed_total(): lax.all_gather(jnp.concatenate([a.ravel() for a in arrays]), axis)  199 us
    all_gather x1, waiting for transfers between devices, shards(): lax.all_gather(out_weight, 'batch', axis=0, tiled=True)  157 us
    all_gather x1, local copies, waits for them, and re-layouts, packed_total(): lax.all_gather(jnp.concatenate([a.ravel() for a in arrays]), axis)  34.4 us
    reduce_sum x1, other arithmetic, packed_total(): jnp.sum(lax.all_gather(jnp.concatenate([a.ravel() for a in arrays]), axis...  16.6 us
    dot_general x1, matrix products, shards(): jnp.einsum('btw,wv->btv', mixed, lax.all_gather(out_weight, 'batch', axis...  14.1 us
  transfers between devices with their start and end apart: 2, of which 2 were waited for; matrix products, arithmetic and copies ran while one was open for 12% of the time, Pallas kernels for 0%

profile of v1, /device:TPU:1, one launch (start us, length us, event | category | flops | bytes accessed | tf_op | source)
XLA Modules:
  0.0 446.4 jit_solution(1374833775931833841)
XLA Ops:
  6.5 0.0 copy-start
  6.5 0.0 all-gather.6.cloned.1.call-start
  6.5 2.6 convert_reduce_fusion
  9.1 0.0 copy-done
  9.1 2.5 fusion.15
  11.7 0.3 reshape.70
  12.0 0.1 reshape.71
  12.1 1.1 pad_maximum_fusion
  13.2 0.0 all-gather.6.cloned.1.call-update
  13.2 0.2 all-gather.4.cloned.1.call-start
  13.4 0.5 all-gather.4.cloned.1.call-update
  13.9 198.9 %all-gather.6.cloned.1.call-done = f32[8519680]{0:T(1024)} async-done(((f32[266240]{0:T(1024)}), f32[8519680]{0:T(1024)}) %all-gather.6.cloned.1.call-update) | async-done | bytes 34078736 | tf_op jit(solution)/shard_map/all_gather | solution.py:11
  212.8 34.4 %reshape.74 = f32[32,266240]{1,0:T(8,128)} reshape(f32[8519680]{0:T(1024)} %all-gather.6.cloned.1.call-done) | data formatting | bytes 68157440 | tf_op jit(solution)/shard_map/all_gather | solution.py:11
  247.2 16.6 %reduce_sum.19 = f32[266240]{0:T(1024)S(1)} reduce(f32[32,266240]{1,0:T(8,128)} %reshape.74, f32[]{:T(128)} %constant.4.clone.1), dimensions={0}, to_apply=%region_1.2 | reduce | flops 8253440 | bytes 35143684 | tf_op jit(solution)/shard_map/reduce_sum | solution.py:11
  263.8 0.1 fusion.14
  263.9 0.4 convert_element_type.38
  264.3 0.1 reshape.75
  264.4 0.0 copy-start.2
  264.4 2.6 fusion.19
  267.0 0.0 copy-done.2
  267.0 1.6 fusion.12
  268.6 156.8 %all-gather.4.cloned.1.call-done = bf16[4096,4096]{1,0:T(8,128)(2,1)} async-done(((bf16[256,4096]{1,0:T(8,128)(2,1)}), bf16[4096,4096]{1,0:T(8,128)(2,1)}) %all-gather.4.cloned.1.call-update) | async-done | bytes 33554448 | tf_op jit(solution)/shard_map/all_gather | solution.py:47
  425.4 0.0 copy-start.1
  425.4 14.1 %fusion = bf16[1,128,4096]{2,1,0:T(8,128)(2,1)} fusion(bf16[128,4096]{0,1:T(8,128)(2,1)S(1)} %bitcast.34, bf16[4096,4096]{1,0:T(8,128)(2,1)} %all-gather.4.cloned.1.call-done), kind=kOutput, calls=%fused_computation.3 | convolution fusion | flops 4295491584 | bytes 35651584 | tf_op jit(solution)/shard_map/btw,wv->btv/dot_general | solution.py:44
  439.6 0.0 copy-done.1
  (2 shorter events, 0.0 us)
Async XLA Ops:
  6.5 2.6 copy-start
  6.5 206.3 %all-gather.6.cloned.1.call-start = ((), (), s32[]{:S(2)}) async-start(), calls=%async_computation.1 | async-start | bytes 35143680 | tf_op jit(solution)/shard_map/all_gather | solution.py:11
  13.2 412.3 %all-gather.4.cloned.1.call-start = ((), (), s32[]{:S(2)}) async-start(), calls=%async_computation | async-start | bytes 35651584 | tf_op jit(solution)/shard_map/all_gather | solution.py:47
  264.4 2.6 copy-start.2
  425.4 14.1 %copy-start.1 = (bf16[1,128,64,64]{1,3,2,0:T(8,128)(2,1)S(1)}, bf16[1,128,64,64]{1,3,2,0:T(8,128)(2,1)}, u32[]{:S(2)}) copy-start(bf16[1,128,64,64]{1,3,2,0:T(8,128)(2,1)} %param.6) | copy-start | bytes 3145732
Sparse Core Ops, SparseCore 0:
  13.3 199.4 all-gather.5
  215.9 209.5 all-gather.3
